TPU v7x, 32 devices: a whole 2x2x4 slice. The times are simulated.
32 devices in a mesh: section: 16 (over z, y, core), walk: 2 (over x).
Axes of the slice: x: 2, y: 2, z: 4, core: 2. Of those that a mesh axis runs over, the one named last changes fastest.
Arguments:
- fields: bfloat16 [16, 8, 800], P('section', None, 'walk'), may hold values from -4 to 4
- cholesky_vectors: bfloat16 [800, 200, 200], P('walk'), may hold values from -0.013 to 0.013
- trial_state: float32 [200, 100], replicated, may hold values from -1.6 to 1.6
- deviation: bfloat16 [16, 8, 200, 100], P('section', 'walk'), may hold values from -0.1796875 to 0.1796875
Outputs:
- density: float32 [8, 200, 200], P('walk')
All inputs are finite; a program needn't handle non-finite values.
Results may differ from a plain program's by a relative error of at most 0.0003.
Values sent between devices are 32-bit elements; how exact they have to be, the bound alone decides.
A program may use at most 128 MiB of HBM per device.

v0:
```python
import jax
import jax.numpy as jnp
from jax import lax
from jax.sharding import PartitionSpec as P

TAYLOR = 6
exact_mode = lax.Precision.HIGHEST


def entering(shard, axis, combine, identity):
    size, position = (lax.axis_size(axis), lax.axis_index(axis))
    everything = lax.all_gather(shard, axis)
    start = jnp.broadcast_to(jnp.asarray(identity, shard.dtype), shard.shape)

    def lap(k, before):
        at = size - 1 - k
        reached = at > position
        new = combine(before, everything[at])
        return jnp.where(reached, new, before)

    return lax.fori_loop(0, size, lap, start)


def series_matrix(field_matrix):
    orbitals = field_matrix.shape[-1]
    series_term = jnp.broadcast_to(jnp.eye(orbitals, dtype=jnp.float32), field_matrix.shape)
    summed = series_term
    for degree in range(1, TAYLOR + 1):
        series_term = (
            jnp.einsum("wij,wjk->wik", series_term, field_matrix, precision=exact_mode) / degree
        )
        summed = summed + series_term
    return summed


def solve_normal(factor, right_side):
    return jax.scipy.linalg.cho_solve((factor, True), right_side)


def green_block(left_state, walker):
    intersection = jnp.einsum("wie,wif->wef", left_state, walker, precision=exact_mode)
    normal_matrix = jnp.einsum("wef,weg->wfg", intersection, intersection, precision=exact_mode)
    right_side = jnp.einsum("wef,wie->wfi", intersection, left_state, precision=exact_mode)
    factor = jnp.linalg.cholesky(normal_matrix)
    solved = jax.vmap(solve_normal)(factor, right_side)
    return jnp.einsum("wie,wej->wij", walker, solved, precision=exact_mode)


def body(fields, cholesky_vectors, trial_state, deviation):
    steps_here, walker_count, chol_here = fields.shape
    orbitals = cholesky_vectors.shape[1]
    per_device = deviation.shape[1]
    field_rows = jnp.swapaxes(fields, 0, 1).reshape(walker_count * steps_here, chol_here)
    vector_table = cholesky_vectors.reshape(chol_here, orbitals * orbitals)
    field_matrices = lax.psum_scatter(
        jnp.dot(field_rows, vector_table, preferred_element_type=jnp.float32),
        "walk",
        scatter_dimension=0,
        tiled=True,
    )
    field_matrices = field_matrices.reshape(per_device, steps_here, orbitals, orbitals)
    walkers = trial_state + deviation.astype(jnp.float32)
    section_count = lax.axis_size("section")
    total_steps = steps_here * section_count
    series = [series_matrix(field_matrices[:, 0])]
    identity = jnp.broadcast_to(
        jnp.eye(orbitals, dtype=jnp.float32), (per_device, orbitals, orbitals)
    )
    block_map = identity
    for offset in reversed(range(steps_here)):
        block_map = jnp.einsum("wji,wjk->wik", series[offset], block_map, precision=exact_mode)

    def compose(earlier, later):
        return jnp.einsum("wij,wjk->wik", later, earlier, precision=exact_mode)

    prefix = entering(block_map, "section", compose, identity)
    incoming = jnp.einsum("wij,je->wie", prefix, trial_state, precision=exact_mode)
    left_state = incoming
    running = jnp.zeros((incoming.shape[0], orbitals, orbitals), jnp.float32)
    for offset in reversed(range(steps_here)):
        left_state = jnp.einsum("wji,wje->wie", series[offset], left_state, precision=exact_mode)
        running = running + green_block(left_state, walkers[offset])
    running, leaving = (running, left_state)
    summed = lax.psum(running, "section")
    return summed / total_steps


def solution(mesh):
    in_specs = (
        P("section", None, "walk"),
        P("walk", None, None),
        P(),
        P("section", "walk", None, None),
    )
    out_specs = P("walk", None, None)
    return jax.shard_map(body, mesh=mesh, in_specs=in_specs, out_specs=out_specs, check_vma=False)
```

profile of v0, /device:TPU:0, one launch (start us, length us, event | category | flops | bytes accessed | tf_op | source)
XLA Modules:
  0.0 450.3 jit_solution(12506095595911162128)
XLA Ops:
  6.5 57.5 %reshape.20 = bf16[400,40000]{1,0:T(8,128)(2,1)} reshape(bf16[400,200,200]{2,1,0:T(8,128)(2,1)} %param.7) | data formatting | bytes 64000000 | tf_op jit(solution)/shard_map/reshape | solution.py:54
  64.0 13.4 %fusion.22 = f32[8,40000]{1,0:T(8,128)} fusion(bf16[400,40000]{1,0:T(8,128)(2,1)} %reshape.20, bf16[1,8,400]{2,1,0:T(8,128)(2,1)S(1)} %copy-done), kind=kOutput, calls=%fused_computation.36 | convolution fusion | flops 256000000 | bytes 33286400 | tf_op jit(solution)/shard_map/dot_general | solution.py:56
  77.5 0.6 dynamic-slice
  78.8 46.8 %all-reduce.6.cloned.1.call-done = f32[8,40000]{1,0:T(8,128)} async-done(((f32[8,40000]{1,0:T(8,128)}), f32[8,40000]{1,0:T(8,128)}) %all-reduce.6.cloned.1.call-update) | async-done | bytes 1280016
  125.5 1.4 constant_dynamic-slice_fusion
  126.9 0.7 squeeze_reshape.3
  127.7 0.8 fusion.10
  128.5 0.9 convolution_multiply_fusion.4
  129.5 0.9 convolution_multiply_fusion.3
  130.4 0.9 convolution_multiply_fusion.2
  131.4 0.9 convolution_multiply_fusion.1
  132.3 1.1 fusion.3
  133.5 2.6 fusion.8
  136.1 0.2 all-reduce.4.cloned.1.call-start
  136.4 103.8 %all-gather.3.cloned.1.call-done = f32[64,200,200]{2,1,0:T(8,128)} async-done(((f32[4,200,200]{2,1,0:T(8,128)}), f32[64,200,200]{2,1,0:T(8,128)}) %all-gather.3.cloned.1.call-update) | async-done | bytes 10240016 | tf_op jit(solution)/shard_map/all_gather | solution.py:12
  240.2 34.8 %while.15 = (s32[]{:T(128)}, f32[4,200,200]{2,1,0:T(8,128)S(1)}, s32[]{:T(128)}, f32[16,4,200,200]{3,2,1,0:T(8,128)}, s32[]{:T(128)}, /*index=5*/s32[]{:T(128)}, s32[]{:T(128)}, s32[]{:T(128)}) while((s32[]{:T(128)}, f32[4,200,200]{2,1,0:T(8,128)S(1)}, s32[]{:T(128)}, f32[16,4,200,200]{3,2,1,0:T(8,128)}, s32[]{:T(128)}, /*index=5*/s32[]{:T(128)}, ...), condition=%wide.region_2.3_spmd, body=%wide.region_1.2_spmd.sunk | while | flops 384160000 | bytes 4377745 | solution.py:21
  240.2 0.1 copy.33
  240.3 2.1 convolution_select_fusion.2
  242.5 2.1 convolution_select_fusion.2
  244.7 2.1 convolution_select_fusion.2
  246.8 2.1 convolution_select_fusion.2
  249.0 2.1 convolution_select_fusion.2
  251.2 2.1 convolution_select_fusion.2
  253.3 2.1 convolution_select_fusion.2
  255.5 2.1 convolution_select_fusion.2
  257.7 2.1 convolution_select_fusion.2
  259.9 2.1 convolution_select_fusion.2
  262.0 2.1 convolution_select_fusion.2
  264.2 2.1 convolution_select_fusion.2
  266.4 2.1 convolution_select_fusion.2
  268.6 2.1 convolution_select_fusion.2
  270.7 2.1 convolution_select_fusion.2
  272.9 2.1 convolution_select_fusion.2
  275.0 0.8 fusion.20
  275.8 1.7 fusion.24
  277.5 1.0 fusion.6
  278.5 0.5 fusion.25
  279.1 0.8 fusion.26
  279.8 0.1 copy.16
  280.0 36.7 %custom-call.11 = f32[4,100,100]{2,1,0:T(8,128)S(1)} custom-call(f32[4,100,100]{2,1,0:T(8,128)S(1)} %fusion.16), custom_call_target="Cholesky" | custom-call | tf_op jit(solution)/shard_map/jit(cholesky)/cholesky | solution.py:44
  316.8 0.1 compare_reduce_fusion
  316.9 0.1 select_bitcast_fusion
  317.0 31.0 %custom-call.12 = f32[4,1,100,100]{2,3,1,0:T(8,128)S(1)} custom-call(f32[4,1,100,100]{3,2,1,0:T(8,128)S(1)} %select_bitcast_fusion), custom_call_target="InvertDiagBlocksLowerTriangular" | custom-call | tf_op jit(solution)/shard_map/vmap(jit(_cho_solve))/triangular_solve | solution.py:37
  348.0 0.8 fusion.14
  348.8 0.8 fusion.12
  349.6 1.7 fusion.4
  351.3 90.3 %all-reduce.4.cloned.1.call-done = f32[4,200,200]{2,1,0:T(8,128)} async-done(((f32[4,200,200]{2,1,0:T(8,128)}), f32[4,200,200]{2,1,0:T(8,128)}) %all-reduce.4.cloned.1.call-update) | async-done | bytes 640016 | tf_op jit(solution)/shard_map/psum | solution.py:84
  441.7 2.1 broadcast_multiply_fusion
  (34 shorter events, 1.1 us)
Async XLA Ops:
  6.5 57.5 %copy-start = (bf16[1,8,400]{2,1,0:T(8,128)(2,1)S(1)}, bf16[1,8,400]{2,1,0:T(8,128)(2,1)}, u32[]{:S(2)}) copy-start(bf16[1,8,400]{2,1,0:T(8,128)(2,1)} %param.6) | copy-start | bytes 19204
  6.5 119.0 %all-reduce.6.cloned.1.call-start = ((), (), s32[]{:S(2)}) async-start(), calls=%async_computation.2 | async-start | bytes 2564096
  64.0 13.5 %copy-start.3 = (u32[32]{0:T(128)S(1)}, u32[32]{0:T(128)}, u32[]{:S(2)}) copy-start(u32[32]{0:T(128)} %constant.123) | copy-start | bytes 388
  77.4 162.7 %all-gather.3.cloned.1.call-start = ((), (), s32[]{:S(2)}) async-start(), calls=%async_computation.1 | async-start | bytes 13926400 | tf_op jit(solution)/shard_map/all_gather | solution.py:12
  133.4 141.6 %copy-start.1 = (f32[200,100]{1,0:T(8,128)S(1)}, f32[200,100]{1,0:T(8,128)}, u32[]{:S(2)}) copy-start(f32[200,100]{1,0:T(8,128)} %param.8) | copy-start | bytes 240004
  136.1 141.5 %copy-start.2 = (bf16[1,4,200,100]{3,2,1,0:T(8,128)(2,1)S(1)}, bf16[1,4,200,100]{3,2,1,0:T(8,128)(2,1)}, u32[]{:S(2)}) copy-start(bf16[1,4,200,100]{3,2,1,0:T(8,128)(2,1)} %param.9) | copy-start | bytes 480004
  136.1 305.6 %all-reduce.4.cloned.1.call-start = ((), (), s32[]{:S(2)}) async-start(), calls=%async_computation | async-start | bytes 1638400 | tf_op jit(solution)/shard_map/psum | solution.py:84
Sparse Core Ops, SparseCore 0:
  77.6 47.9 all-reduce.5
  136.2 103.9 all-gather.2
  351.5 90.1 all-reduce.3
where the time goes:
time: 453 us; the launch traced here: 450 us
  waiting for transfers between devices  241 us (53%)
  other arithmetic  70.1 us (15%)
  matrix products  63.1 us (14%)
  local copies, waits for them, and re-layouts  61.3 us (14%)
  between operations  14 us (3%)
    all_gather x1, waiting for transfers between devices, entering(): everything = lax.all_gather(shard, axis)  104 us
    psum x1, waiting for transfers between devices, body(): summed = lax.psum(running, 'section')  90.3 us
    reshape x1, local copies, waits for them, and re-layouts, body(): vector_table = cholesky_vectors.reshape(chol_here, orbitals * orbitals)  57.5 us
    unnamed x4, waiting for transfers between devices  46.8 us
    another operation x4, other arithmetic, green_block(): factor = jnp.linalg.cholesky(normal_matrix)  36.9 us
    dot_general x16, matrix products, compose(): return jnp.einsum('wij,wjk->wik', later, earlier, precision=exact_mode)  33.2 us
    another operation x3, other arithmetic, solve_normal(): return jax.scipy.linalg.cho_solve((factor, True), right_side)  31.1 us
    dot_general x1, matrix products, body(): jnp.dot(field_rows, vector_table, preferred_element_type=jnp.float32)  13.4 us
  transfers between devices with their start and end apart: 3, of which 3 were waited for; matrix products, arithmetic and copies ran while one was open for 0% of the time, Pallas kernels for 0%

commit v1 on v0

--- a/solution.py
+++ b/solution.py
@@ -81,7 +81,9 @@
         left_state = jnp.einsum("wji,wje->wie", series[offset], left_state, precision=exact_mode)
         running = running + green_block(left_state, walkers[offset])
     running, leaving = (running, left_state)
-    summed = lax.psum(running, "section")
+    summed = running
+    for hop in (1, 2, 4, 8):
+        summed = summed + lax.ppermute(summed, "section", [(dev, dev ^ hop) for dev in range(16)])
     return summed / total_steps
 
 

time: 453 us -> 441 us (0.974)
  waiting for transfers between devices: 241 us -> 227 us
    psum x1 -> x0, waiting for transfers between devices: 90.3 us -> none  [body(): summed = lax.psum(running, 'section')]
    ppermute x0 -> x4, waiting for transfers between devices: none -> 76.6 us  [body(): lax.ppermute(summed, 'section', [(dev, dev ^ hop) for dev in range(16)])]
    unnamed x4 -> x3, waiting for transfers between devices: 46.8 us -> 46.8 us
  transfers between devices with their start and end apart: 3 -> 6, of which waited for: 3 -> 6; matrix products, arithmetic and copies ran while one was open for 0% -> 0% of each run, Pallas kernels for 0% -> 0%
where the time goes in v1:
time: 441 us; the launch traced here: 438 us
  waiting for transfers between devices  227 us (51%)
  other arithmetic  69.3 us (16%)
  matrix products  62.2 us (14%)
  local copies, waits for them, and re-layouts  61.3 us (14%)
  between operations  14.3 us (3%)
    all_gather x1, waiting for transfers between devices, entering(): everything = lax.all_gather(shard, axis)  104 us
    ppermute x4, waiting for transfers between devices, body(): lax.ppermute(summed, 'section', [(dev, dev ^ hop) for dev in range(16)])  76.6 us
    reshape x1, local copies, waits for them, and re-layouts, body(): vector_table = cholesky_vectors.reshape(chol_here, orbitals * orbitals)  57.5 us
    unnamed x3, waiting for transfers between devices  46.8 us
    another operation x4, other arithmetic, green_block(): factor = jnp.linalg.cholesky(normal_matrix)  36.9 us
    dot_general x16, matrix products, compose(): return jnp.einsum('wij,wjk->wik', later, earlier, precision=exact_mode)  33.2 us
    another operation x3, other arithmetic, solve_normal(): return jax.scipy.linalg.cho_solve((factor, True), right_side)  31.1 us
    dot_general x1, matrix products, body(): jnp.dot(field_rows, vector_table, preferred_element_type=jnp.float32)  13.4 us
  transfers between devices with their start and end apart: 6, of which 6 were waited for; matrix products, arithmetic and copies ran while one was open for 0% of the time, Pallas kernels for 0%

profile of v1, /device:TPU:0, one launch (start us, length us, event | category | flops | bytes accessed | tf_op | source)
XLA Modules:
  0.0 438.3 jit_solution(12323695519759260663)
XLA Ops:
  6.5 57.5 %reshape.20 = bf16[400,40000]{1,0:T(8,128)(2,1)} reshape(bf16[400,200,200]{2,1,0:T(8,128)(2,1)} %param.7) | data formatting | bytes 64000000 | tf_op jit(solution)/shard_map/reshape | solution.py:54
  64.0 13.4 %fusion.22 = f32[8,40000]{1,0:T(8,128)} fusion(bf16[400,40000]{1,0:T(8,128)(2,1)} %reshape.20, bf16[1,8,400]{2,1,0:T(8,128)(2,1)S(1)} %copy-done), kind=kOutput, calls=%fused_computation.36 | convolution fusion | flops 256000000 | bytes 33286400 | tf_op jit(solution)/shard_map/dot_general | solution.py:56
  77.5 0.6 dynamic-slice
  78.8 46.8 %all-reduce.3.cloned.1.call-done = f32[8,40000]{1,0:T(8,128)} async-done(((f32[8,40000]{1,0:T(8,128)}), f32[8,40000]{1,0:T(8,128)}) %all-reduce.3.cloned.1.call-update) | async-done | bytes 1280016
  125.5 1.4 constant_dynamic-slice_fusion
  126.9 0.7 squeeze_reshape.3
  127.7 0.8 fusion.10
  128.5 0.9 convolution_multiply_fusion.4
  129.5 0.9 convolution_multiply_fusion.3
  130.4 0.9 convolution_multiply_fusion.2
  131.4 0.9 convolution_multiply_fusion.1
  132.3 1.1 fusion.3
  133.5 2.6 fusion.8
  136.1 104.0 %all-gather.3.cloned.1.call-done = f32[64,200,200]{2,1,0:T(8,128)} async-done(((f32[4,200,200]{2,1,0:T(8,128)}), f32[64,200,200]{2,1,0:T(8,128)}) %all-gather.3.cloned.1.call-update) | async-done | bytes 10240016 | tf_op jit(solution)/shard_map/all_gather | solution.py:12
  240.2 35.0 %while.15 = (s32[]{:T(128)}, f32[4,200,200]{2,1,0:T(8,128)S(1)}, s32[]{:T(128)}, f32[16,4,200,200]{3,2,1,0:T(8,128)}, s32[]{:T(128)}, /*index=5*/s32[]{:T(128)}, s32[]{:T(128)}, s32[]{:T(128)}) while((s32[]{:T(128)}, f32[4,200,200]{2,1,0:T(8,128)S(1)}, s32[]{:T(128)}, f32[16,4,200,200]{3,2,1,0:T(8,128)}, s32[]{:T(128)}, /*index=5*/s32[]{:T(128)}, ...), condition=%wide.region_2.3_spmd, body=%wide.region_1.2_spmd.sunk | while | flops 384160000 | bytes 4377745 | solution.py:21
  240.5 2.1 convolution_select_fusion.2
  242.7 2.1 convolution_select_fusion.2
  244.8 2.1 convolution_select_fusion.2
  247.0 2.1 convolution_select_fusion.2
  249.2 2.1 convolution_select_fusion.2
  251.4 2.1 convolution_select_fusion.2
  253.5 2.1 convolution_select_fusion.2
  255.7 2.1 convolution_select_fusion.2
  257.9 2.1 convolution_select_fusion.2
  260.1 2.1 convolution_select_fusion.2
  262.2 2.1 convolution_select_fusion.2
  264.4 2.1 convolution_select_fusion.2
  266.6 2.1 convolution_select_fusion.2
  268.8 2.1 convolution_select_fusion.2
  270.9 2.1 convolution_select_fusion.2
  273.1 2.1 convolution_select_fusion.2
  275.2 0.8 fusion.20
  276.0 1.7 fusion.24
  277.7 1.0 fusion.6
  278.7 0.5 fusion.25
  279.3 0.8 fusion.26
  280.2 36.7 %custom-call.11 = f32[4,100,100]{2,1,0:T(8,128)S(1)} custom-call(f32[4,100,100]{2,1,0:T(8,128)S(1)} %fusion.16), custom_call_target="Cholesky" | custom-call | tf_op jit(solution)/shard_map/jit(cholesky)/cholesky | solution.py:44
  317.2 31.0 %custom-call.12 = f32[4,1,100,100]{2,3,1,0:T(8,128)S(1)} custom-call(f32[4,1,100,100]{3,2,1,0:T(8,128)S(1)} %select_bitcast_fusion), custom_call_target="InvertDiagBlocksLowerTriangular" | custom-call | tf_op jit(solution)/shard_map/vmap(jit(_cho_solve))/triangular_solve | solution.py:37
  348.2 0.8 fusion.14
  349.0 0.8 fusion.12
  349.8 0.8 fusion.4
  351.0 2.1 collective-permute-done
  353.2 0.6 collective-permute-start.1
  353.8 19.8 %collective-permute-done.1 = f32[4,200,200]{2,1,0:T(8,128)S(1)} collective-permute-done((f32[4,200,200]{2,1,0:T(8,128)S(1)}, f32[4,200,200]{2,1,0:T(8,128)S(1)}, u32[]{:S(2)}, u32[]{:S(2)}) %collective-permute-start.1) | collective-permute-done | bytes 640032 | tf_op jit(solution)/shard_map/ppermute | solution.py:86
  374.1 19.2 %collective-permute-done.2 = f32[4,200,200]{2,1,0:T(8,128)S(1)} collective-permute-done((f32[4,200,200]{2,1,0:T(8,128)S(1)}, f32[4,200,200]{2,1,0:T(8,128)S(1)}, u32[]{:S(2)}, u32[]{:S(2)}) %collective-permute-start.2) | collective-permute-done | bytes 640032 | tf_op jit(solution)/shard_map/ppermute | solution.py:86
  393.5 1.5 collective-permute-start.3
  395.0 35.4 %collective-permute-done.3 = f32[4,200,200]{2,1,0:T(8,128)S(1)} collective-permute-done((f32[4,200,200]{2,1,0:T(8,128)S(1)}, f32[4,200,200]{2,1,0:T(8,128)S(1)}, u32[]{:S(2)}, u32[]{:S(2)}) %collective-permute-start.3) | collective-permute-done | bytes 640032 | tf_op jit(solution)/shard_map/ppermute | solution.py:86
  430.4 1.0 add_multiply_fusion
  (44 shorter events, 2.6 us)
Async XLA Ops:
  6.5 57.5 %copy-start = (bf16[1,8,400]{2,1,0:T(8,128)(2,1)S(1)}, bf16[1,8,400]{2,1,0:T(8,128)(2,1)}, u32[]{:S(2)}) copy-start(bf16[1,8,400]{2,1,0:T(8,128)(2,1)} %param.6) | copy-start | bytes 19204
  6.5 119.0 %all-reduce.3.cloned.1.call-start = ((), (), s32[]{:S(2)}) async-start(), calls=%async_computation.1 | async-start | bytes 2564096
  64.0 13.5 %copy-start.4 = (u32[32]{0:T(128)S(1)}, u32[32]{0:T(128)}, u32[]{:S(2)}) copy-start(u32[32]{0:T(128)} %constant.123) | copy-start | bytes 388
  77.4 162.7 %all-gather.3.cloned.1.call-start = ((), (), s32[]{:S(2)}) async-start(), calls=%async_computation | async-start | bytes 13926400 | tf_op jit(solution)/shard_map/all_gather | solution.py:12
  133.5 141.8 %copy-start.2 = (f32[200,100]{1,0:T(8,128)S(1)}, f32[200,100]{1,0:T(8,128)}, u32[]{:S(2)}) copy-start(f32[200,100]{1,0:T(8,128)} %param.8) | copy-start | bytes 240004
  136.1 141.7 %copy-start.3 = (bf16[1,4,200,100]{3,2,1,0:T(8,128)(2,1)S(1)}, bf16[1,4,200,100]{3,2,1,0:T(8,128)(2,1)}, u32[]{:S(2)}) copy-start(bf16[1,4,200,100]{3,2,1,0:T(8,128)(2,1)} %param.9) | copy-start | bytes 480004
  275.2 156.2 %copy-start.1 = (bf16[1,8,400]{2,1,0:T(8,128)(2,1)S(1)}, bf16[1,8,400]{2,1,0:T(8,128)(2,1)}, u32[]{:S(2)}) copy-start(bf16[1,8,400]{2,1,0:T(8,128)(2,1)} %param.6) | copy-start | bytes 19204
  350.6 2.4 collective-permute-start
  353.2 20.5 %collective-permute-start.1 = (f32[4,200,200]{2,1,0:T(8,128)S(1)}, f32[4,200,200]{2,1,0:T(8,128)S(1)}, u32[]{:S(2)}, u32[]{:S(2)}) collective-permute-start(f32[4,200,200]{2,1,0:T(8,128)S(1)} %add.94), channel_id=1, source_target_pairs={{0,4},{2,6},{4,0},{6,2},{8,12},{10,14},{12,8},{14,10},{16,20},{18,... | collective-permute-start | bytes 1920008 | tf_op jit(solution)/shard_map/ppermute | solution.py:86
  373.7 19.6 %collective-permute-start.2 = (f32[4,200,200]{2,1,0:T(8,128)S(1)}, f32[4,200,200]{2,1,0:T(8,128)S(1)}, u32[]{:S(2)}, u32[]{:S(2)}) collective-permute-start(f32[4,200,200]{2,1,0:T(8,128)S(1)} %add.95), channel_id=1, source_target_pairs={{0,8},{2,10},{4,12},{6,14},{8,0},{10,2},{12,4},{14,6},{16,24},{18,... | collective-permute-start | bytes 1920008 | tf_op jit(solution)/shard_map/ppermute | solution.py:86
  393.5 37.0 %collective-permute-start.3 = (f32[4,200,200]{2,1,0:T(8,128)S(1)}, f32[4,200,200]{2,1,0:T(8,128)S(1)}, u32[]{:S(2)}, u32[]{:S(2)}) collective-permute-start(f32[4,200,200]{2,1,0:T(8,128)S(1)} %add.96), channel_id=1, source_target_pairs={{0,16},{2,18},{4,20},{6,22},{8,24},{10,26},{12,28},{14,30},{16,0},... | collective-permute-start | bytes 1920008 | tf_op jit(solution)/shard_map/ppermute | solution.py:86
Sparse Core Ops, SparseCore 0:
  77.6 47.9 all-reduce.2
  136.2 103.9 all-gather.2
